TPU v7x, 32 devices: a whole 2x2x4 slice. The times are simulated.
32 devices in a mesh: row: 8 (over y, x, core), col: 4 (over z).
Axes of the slice: x: 2, y: 2, z: 4, core: 2. Of those that a mesh axis runs over, the one named last changes fastest.
Arguments:
- history: float32 [3, 512, 4096], P(None, None, ('row', 'col')), may hold values from -8 to 8
Outputs:
- orbitals: float32 [512, 4096], P(None, ('row', 'col'))
All inputs are finite; a program needn't handle non-finite values.
Results may differ from a plain program's by a relative error of at most 0.0003.
Values sent between devices are 32-bit elements; how exact they have to be, the bound alone decides.
A program may use at most 64 MiB of HBM per device.

v0:
```python
import jax
import jax.numpy as jnp
from jax import lax
from jax.sharding import PartitionSpec as P


def on_device(history):
    precise = lax.Precision.HIGHEST
    npw_total = history.shape[2] * lax.axis_size("row") * lax.axis_size("col")
    newest = history[0]
    local_terms = tuple(
        (jnp.einsum("ip,jp->ij", newest, history[index], precision=precise) for index in range(3))
    )
    summed = lax.psum(local_terms, ("row", "col"))
    weights = (2.5, -2.0, 0.5)
    predicted = jnp.zeros(newest.shape, jnp.float32)
    for index in range(3):
        project = summed[index] / npw_total
        predicted = predicted + weights[index] * jnp.dot(project, history[index], precision=precise)
    local_gram = jnp.einsum("ip,jp->ij", predicted, predicted, precision=precise)
    gram = lax.psum(local_gram, ("row", "col"))
    factor = jnp.linalg.cholesky(gram / npw_total)
    return lax.linalg.triangular_solve(factor, predicted, left_side=True, lower=True)


def solution(mesh):
    return jax.shard_map(
        on_device,
        mesh=mesh,
        in_specs=(P(None, None, ("row", "col")),),
        out_specs=P(None, ("row", "col")),
        check_vma=False,
    )
```

profile of v0, /device:TPU:0, one launch (start us, length us, event | category | flops | bytes accessed | tf_op | source)
XLA Modules:
  0.0 441.6 jit_solution(1607792850113480831)
XLA Ops:
  6.5 3.1 fusion.11
  9.7 2.0 fusion.14
  11.6 2.0 fusion.19
  13.6 0.2 all-reduce.5.cloned.1.call-start
  13.9 141.6 %all-reduce.7.cloned.1.call-done = (f32[512,512]{0,1:T(8,128)}, f32[512,512]{0,1:T(8,128)}, f32[512,512]{0,1:T(8,128)}) async-done(((f32[512,512]{0,1:T(8,128)}, f32[512,512]{0,1:T(8,128)}, f32[512,512]{0,1:T(8,128)}), (f32[512,512]{0,1:T(8,128)}, f32[512,512]{0,1:T(8,128)}, f32[512,512]{0,1:T(8,128)})) %all-reduce.7.cloned.1.call-update) | async-done | bytes 3145744 | tf_op jit(solution)/shard_map/psum | solution.py:14
  155.4 3.1 convolution_multiply_fusion.2
  158.6 1.8 fusion.1
  160.4 1.8 fusion
  162.2 2.0 fusion.61
  164.3 130.2 %all-reduce.5.cloned.1.call-done = f32[512,512]{0,1:T(8,128)} async-done(((f32[512,512]{0,1:T(8,128)}), f32[512,512]{0,1:T(8,128)}) %all-reduce.5.cloned.1.call-update) | async-done | bytes 1048592 | tf_op jit(solution)/shard_map/psum | solution.py:21
  294.5 1.3 broadcast_multiply_fusion
  295.8 0.3 copy.3
  296.2 0.9 copy-done.1
  297.0 0.2 fusion.2
  297.3 11.7 %cholesky.104 = f32[128,128]{1,0:T(8,128)S(1)} custom-call(f32[128,128]{1,0:T(8,128)S(1)} %cholesky.266), custom_call_target="Cholesky" | custom-call | tf_op jit(solution)/shard_map/jit(cholesky)/cholesky | solution.py:22
  309.0 10.0 %custom-call.30 = f32[1,128,128]{1,2,0:T(8,128)S(1)} custom-call(f32[1,128,128]{2,1,0:T(8,128)S(1)} %get-tuple-element.35), custom_call_target="InvertDiagBlocksLowerTriangular" | custom-call | tf_op jit(solution)/shard_map/jit(cholesky)/cholesky | solution.py:22
  319.2 0.3 constant_dynamic-update-slice_fusion.3
  319.5 0.3 convolution_subtract_fusion
  319.8 11.7 %cholesky.217 = f32[128,128]{1,0:T(8,128)S(1)} custom-call(f32[128,128]{1,0:T(8,128)S(1)} %cholesky.270), custom_call_target="Cholesky" | custom-call | tf_op jit(solution)/shard_map/jit(cholesky)/cholesky | solution.py:22
  331.6 9.8 %custom-call.31 = f32[1,128,128]{1,2,0:T(8,128)S(1)} custom-call(f32[1,128,128]{2,1,0:T(8,128)S(1)} %get-tuple-element.32), custom_call_target="InvertDiagBlocksLowerTriangular" | custom-call | tf_op jit(solution)/shard_map/jit(cholesky)/cholesky | solution.py:22
  341.4 0.3 convolution_dynamic-update-slice_fusion
  341.7 0.4 convolution_subtract_fusion.1
  342.1 11.7 %cholesky.238 = f32[128,128]{1,0:T(8,128)S(1)} custom-call(f32[128,128]{1,0:T(8,128)S(1)} %cholesky.275), custom_call_target="Cholesky" | custom-call | tf_op jit(solution)/shard_map/jit(cholesky)/cholesky | solution.py:22
  353.8 0.7 compare_reduce_fusion.1
  354.5 10.0 %custom-call.32 = f32[1,128,128]{1,2,0:T(8,128)S(1)} custom-call(f32[1,128,128]{2,1,0:T(8,128)S(1)} %get-tuple-element.29), custom_call_target="InvertDiagBlocksLowerTriangular" | custom-call | tf_op jit(solution)/shard_map/jit(cholesky)/cholesky | solution.py:22
  364.6 0.2 convolution_dynamic-update-slice_fusion.1
  364.8 0.4 convolution_subtract_fusion.5
  365.2 11.7 %cholesky.255 = f32[128,128]{1,0:T(8,128)S(1)} custom-call(f32[128,128]{1,0:T(8,128)S(1)} %convolution_subtract_fusion.5), custom_call_target="Cholesky" | custom-call | tf_op jit(solution)/shard_map/jit(cholesky)/cholesky | solution.py:22
  376.9 0.6 compare_reduce_fusion
  377.6 0.7 compare_reduce_fusion.2
  380.9 10.6 %while.1 = (s32[]{:T(128)}, f32[512,512]{1,0:T(8,128)S(1)}, s32[4,2]{0,1:T(2,128)S(1)}, f32[4,128,128]{2,1,0:T(8,128)}, s32[]{:T(128)}) while((s32[]{:T(128)}, f32[512,512]{1,0:T(8,128)S(1)}, s32[4,2]{0,1:T(2,128)S(1)}, f32[4,128,128]{2,1,0:T(8,128)}, s32[]{:T(128)}) %tuple.27), condition=%wide.while_cond, body=%wide.while_body.sunk | while | flops 2 | bytes 132705 | solution.py:23
  381.0 0.6 fusion.70
  381.6 2.0 bitcast_dynamic-update-slice_fusion.2
  383.7 0.6 fusion.70
  384.3 2.0 bitcast_dynamic-update-slice_fusion.2
  386.3 0.6 fusion.70
  386.9 2.0 bitcast_dynamic-update-slice_fusion.2
  388.9 0.6 fusion.70
  389.6 2.0 bitcast_dynamic-update-slice_fusion.2
  391.5 40.1 %custom-call.33 = f32[4,128,128]{1,2,0:T(8,128)S(1)} custom-call(f32[4,128,128]{2,1,0:T(8,128)} %get-tuple-element.12), custom_call_target="InvertDiagBlocksLowerTriangular" | custom-call | tf_op jit(solution)/shard_map/triangular_solve | solution.py:23
  431.7 0.3 fusion.48
  431.9 0.2 convolution_subtract_fusion.3
  432.2 0.3 fusion.47
  432.4 0.3 convolution_subtract_fusion.2
  432.7 0.3 fusion.45
  433.0 0.3 convolution_subtract_fusion.4
  433.3 0.3 fusion.44
  433.6 0.7 pad_maximum_fusion
  (26 shorter events, 0.8 us)
Async XLA Ops:
  6.5 3.1 copy-start
  6.5 148.9 %all-reduce.7.cloned.1.call-start = ((), (), s32[]{:S(2)}) async-start(), calls=%async_computation.1 | async-start | bytes 6291456 | tf_op jit(solution)/shard_map/psum | solution.py:14
  13.6 280.9 %all-reduce.5.cloned.1.call-start = ((), (), s32[]{:S(2)}) async-start(), calls=%async_computation | async-start | bytes 2097152 | tf_op jit(solution)/shard_map/psum | solution.py:21
  155.4 3.1 copy-start.3
  158.5 1.8 copy-start.2
  295.8 1.2 copy-start.1
Sparse Core Ops, SparseCore 0:
  13.8 141.6 all-reduce.6
  164.4 130.0 all-reduce.4
where the time goes:
time: 445 us; the launch traced here: 442 us
  waiting for transfers between devices  272 us (61%)
  other arithmetic  121 us (27%)
  matrix products  19.7 us (4%)
  between operations  16.6 us (4%)
  local copies, waits for them, and re-layouts  11.9 us (3%)
    psum x1, waiting for transfers between devices, on_device(): summed = lax.psum(local_terms, ('row', 'col'))  142 us
    psum x1, waiting for transfers between devices, on_device(): gram = lax.psum(local_gram, ('row', 'col'))  130 us
    another operation x14, other arithmetic, on_device(): factor = jnp.linalg.cholesky(gram / npw_total)  78.9 us
    another operation x4, other arithmetic, on_device(): lax.linalg.triangular_solve(factor, predicted, left_side=True, lower=True)  41 us
    another operation x12, local copies, waits for them, and re-layouts  10.6 us
  transfers between devices with their start and end apart: 2, of which 2 were waited for; matrix products, arithmetic and copies ran while one was open for 0% of the time, Pallas kernels for 0%

commit v1 on v0

v1 whole, which is shorter than its diff:
```python
import functools

import jax
import jax.numpy as jnp
import numpy as np
from jax import lax
from jax.experimental import pallas as pl
from jax.experimental.pallas import tpu as pltpu
from jax.sharding import PartitionSpec as P

MESH = pl.DeviceIdType.MESH
B = 128
STREAMS = 3
WEIGHTS = (2.5, -2.0, 0.5)
NT = (((1,), (1,)), ((), ()))
NN = (((1,), (0,)), ((), ()))


def split(x):
    high = x.astype(jnp.bfloat16)
    return high, (x - high.astype(jnp.float32)).astype(jnp.bfloat16)


def dot3(a, b, dims):
    mul = functools.partial(lax.dot_general, dimension_numbers=dims, preferred_element_type=jnp.float32)
    return mul(a[0], b[0]) + (mul(a[0], b[1]) + mul(a[1], b[0]))


def exchange_orders(n_row, n_col):
    row = [("row", bit) for bit in range(1, n_row.bit_length() - 1)]
    col = [("col", bit) for bit in range(n_col.bit_length() - 1)]
    half = (len(row) + 1) // 2
    parts = [row[:half], row[half:], col]
    first = [("row", 0)]
    return [first + parts[s] + parts[(s + 1) % 3] + parts[(s + 2) % 3] for s in range(STREAMS)]


def plan(rows, stages, halvings):
    steps, offset = [], 0
    for stage in range(stages):
        halve = stage < halvings and rows % 16 == 0 and rows >= 16
        if halve:
            rows //= 2
        steps.append((halve, rows, offset))
        offset += rows
    return steps, offset


def layout(blocks):
    place, counts = {}, []
    for stream, part in enumerate(np.array_split(np.arange(len(blocks)), STREAMS)):
        counts.append(len(part))
        for slot, index in enumerate(part):
            place[blocks[index]] = (stream, slot * B)
    return place, counts


def projection_blocks(nb):
    return [(0, i, k) for i in range(nb) for k in range(i + 1)] + [
        (j, i, k) for j in (1, 2) for i in range(nb) for k in range(nb)
    ]


def gram_blocks(nb):
    return [(i, k) for i in range(nb) for k in range(i + 1)]


class Reducer:
    def __init__(self, accs, recvs, sums, send_sem, recv_sem, gsend_sem, grecv_sem, orders, plans):
        self.accs, self.recvs, self.sums, self.orders, self.plans = accs, recvs, sums, orders, plans
        self.sems = (send_sem, recv_sem, gsend_sem, grecv_sem)
        self.off = [0] * len(accs)
        self.parent = [[] for _ in accs]
        self.copies = {}
        self.index = {axis: lax.axis_index(axis) for axis in ("row", "col")}

    def partner(self, axis, bit):
        me = self.index[axis]
        side = lax.rem(lax.div(me, 1 << bit), 2)
        other = me + (1 - 2 * side) * (1 << bit)
        device = (other, self.index["col"]) if axis == "row" else (self.index["row"], other)
        return side, device

    def start(self, s, t):
        side, device = self.partner(*self.orders[s][t])
        halve, rows, at = self.plans[s][t]
        off = self.off[s]
        self.parent[s].append(off)
        sent = off
        if halve:
            sent = pl.multiple_of(off + (1 - side) * rows, 8)
            self.off[s] = pl.multiple_of(off + side * rows, 8)
        copy = pltpu.make_async_remote_copy(
            src_ref=self.accs[s].at[pl.ds(sent, rows)],
            dst_ref=self.recvs[s].at[pl.ds(at, rows)],
            send_sem=self.sems[0].at[s, t],
            recv_sem=self.sems[1].at[s, t],
            device_id=device,
            device_id_type=MESH,
        )
        copy.start()
        self.copies[s] = copy

    def finish(self, s, t):
        self.copies[s].wait()
        _, rows, at = self.plans[s][t]
        here = pl.ds(self.off[s], rows)
        target = self.sums[s] if t + 1 == len(self.orders[s]) else self.accs[s]
        target[here] = self.accs[s][here] + self.recvs[s][pl.ds(at, rows)]

    def run(self):
        stages = len(self.orders[0])
        streams = range(len(self.accs))
        for t in range(stages):
            for s in streams:
                self.finish(s, t)
                if t + 1 < stages:
                    self.start(s, t + 1)
        for t in reversed(range(stages)):
            for s in streams:
                halve, rows, _ = self.plans[s][t]
                if not halve:
                    continue
                _, device = self.partner(*self.orders[s][t])
                here = pl.ds(self.off[s], rows)
                copy = pltpu.make_async_remote_copy(
                    src_ref=self.sums[s].at[here],
                    dst_ref=self.sums[s].at[here],
                    send_sem=self.sems[2].at[s, t],
                    recv_sem=self.sems[3].at[s, t],
                    device_id=device,
                    device_id_type=MESH,
                )
                copy.start()
                self.copies[s] = copy
            for s in streams:
                if self.plans[s][t][0]:
                    self.copies[s].wait()
                    self.off[s] = self.parent[s][t]


def predict_kernel(npw, orders, m_plans, g_plans, h_ref, p_ref, g_ref, *scratch):
    m_acc, scratch = scratch[:STREAMS], scratch[STREAMS:]
    m_recv, scratch = scratch[:STREAMS], scratch[STREAMS:]
    m_sum, scratch = scratch[:STREAMS], scratch[STREAMS:]
    g_acc, scratch = scratch[:STREAMS], scratch[STREAMS:]
    g_recv, scratch = scratch[:STREAMS], scratch[STREAMS:]
    g_sum, sems = scratch[:STREAMS], scratch[STREAMS:]
    nb = h_ref.shape[1] // B
    m_red = Reducer(m_acc, m_recv, m_sum, *sems[:4], orders, m_plans)
    g_red = Reducer(g_acc, g_recv, g_sum, *sems[4:], orders, g_plans)

    barrier = pltpu.get_barrier_semaphore()
    for axis, bit in orders[0]:
        pl.semaphore_signal(barrier, inc=1, device_id=m_red.partner(axis, bit)[1], device_id_type=MESH)

    hist = [split(h_ref[j]) for j in range(3)]
    place, counts = layout(projection_blocks(nb))
    left = list(counts)
    waited = False
    for j in range(3):
        for i in range(nb):
            width = (i + 1) * B if j == 0 else nb * B
            mine = tuple(x[i * B : (i + 1) * B] for x in hist[0])
            other = tuple(x[:width] for x in hist[j])
            product = dot3(mine, other, NT)
            for k in range(width // B):
                stream, row = place[(j, i, k)]
                m_acc[stream][row : row + B, :] = product[:, k * B : (k + 1) * B]
                left[stream] -= 1
                if left[stream] == 0:
                    if not waited:
                        pl.semaphore_wait(barrier, len(orders[0]))
                        waited = True
                    m_red.start(stream, 0)
    m_red.run()

    def block(j, i, k):
        if j == 0 and k > i:
            return jnp.transpose(block(0, k, i))
        stream, row = place[(j, i, k)]
        return m_sum[stream][row : row + B, :]

    scaled = split(jnp.concatenate([h_ref[j] * (WEIGHTS[j] / npw) for j in range(3)], axis=0))
    g_place, g_counts = layout(gram_blocks(nb))
    left = list(g_counts)
    highs, lows = [], []
    for i in range(nb):
        line = jnp.concatenate([block(j, i, k) for j in range(3) for k in range(nb)], axis=1)
        predicted = dot3(split(line), scaled, NN)
        p_ref[i * B : (i + 1) * B, :] = predicted
        high, low = split(predicted)
        highs.append(high)
        lows.append(low)
        others = (jnp.concatenate(highs, axis=0), jnp.concatenate(lows, axis=0))
        product = dot3((high, low), others, NT)
        for k in range(i + 1):
            stream, row = g_place[(i, k)]
            g_acc[stream][row : row + B, :] = product[:, k * B : (k + 1) * B]
            left[stream] -= 1
            if left[stream] == 0:
                g_red.start(stream, 0)
    g_red.run()
    row = 0
    for stream in range(STREAMS):
        rows = g_counts[stream] * B
        g_ref[row : row + rows, :] = g_sum[stream][...] * (1.0 / npw)
        row += rows


def inverse_factor(tile, work):
    rows_of = lax.broadcasted_iota(jnp.int32, (B, B), 0)
    cols_of = lax.broadcasted_iota(jnp.int32, (B, B), 1)
    work[:, :B] = tile
    work[:, B:] = jnp.where(rows_of == cols_of, 1.0, 0.0)
    sub = lax.broadcasted_iota(jnp.int32, (8, B), 0)
    inverse = []
    for k in range(0, B, 8):
        left, right = work[k : k + 8, :B], work[k : k + 8, B:]
        cols = [jnp.broadcast_to(left[:, k + r : k + r + 1], (8, B)) for r in range(8)]
        pivots = None
        for r in range(8):
            def line(x):
                return jnp.broadcast_to(x[r : r + 1, :], (8, B))

            pivot = line(cols[r])
            pivots = pivot if r == 0 else jnp.where(sub == r, pivot, pivots)
            if r < 7:
                scale = jnp.where(sub > r, cols[r] / pivot, 0.0)
                for s in range(r + 1, 8):
                    cols[s] = cols[s] - scale * line(cols[s])
                left = left - scale * line(left)
                right = right - scale * line(right)
        root = 1.0 / jnp.sqrt(pivots)
        left, right = left * root, right * root
        inverse.append(right)
        if k + 8 < B:
            lh = left.astype(jnp.bfloat16).astype(jnp.float32)
            rh = right.astype(jnp.bfloat16).astype(jnp.float32)
            ll, rl = left - lh, right - rh
            zero = jnp.zeros_like(lh)
            tall = jnp.transpose(jnp.concatenate([lh, ll, lh, zero], axis=0)).astype(jnp.bfloat16)
            wide = jnp.concatenate(
                [jnp.concatenate([lh, lh, ll, zero], axis=0), jnp.concatenate([rh, rh, rl, zero], axis=0)], axis=1
            ).astype(jnp.bfloat16)
            update = lax.dot_general(tall, wide, NN, preferred_element_type=jnp.float32)
            work[k + 8 :, :] = work[k + 8 :, :] - update[k + 8 :, :]
    return jnp.concatenate(inverse, axis=0)


def solve_kernel(p_ref, g_ref, out_ref, gram, rest, work):
    nb = p_ref.shape[0] // B
    place = {block: index * B for index, block in enumerate(gram_blocks(nb))}
    gram[...] = g_ref[...]
    rest[...] = p_ref[...]

    def tile(ref, row):
        return ref.at[row : row + B]

    for k in range(nb):
        inverse = split(inverse_factor(tile(gram, place[(k, k)])[...], work))
        solved = dot3(inverse, split(tile(rest, k * B)[...]), NN)
        tile(out_ref, k * B)[...] = solved
        solved = split(solved)
        panel = {i: split(dot3(split(tile(gram, place[(i, k)])[...]), inverse, NT)) for i in range(k + 1, nb)}
        for i in range(k + 1, nb):
            here = tile(rest, i * B)
            here[...] = here[...] - dot3(panel[i], solved, NN)
            for j in range(k + 1, i + 1):
                here = tile(gram, place[(i, j)])
                here[...] = here[...] - dot3(panel[i], panel[j], NT)


def on_device(history):
    n_row, n_col = lax.axis_size("row"), lax.axis_size("col")
    norb, width = history.shape[1:]
    npw = width * n_row * n_col
    nb = norb // B
    orders = exchange_orders(n_row, n_col)
    stages = len(orders[0])
    m_counts = layout(projection_blocks(nb))[1]
    g_counts = layout(gram_blocks(nb))[1]
    m_plans = [plan(count * B, stages, 4) for count in m_counts]
    g_plans = [plan(count * B, stages, 2) for count in g_counts]
    f32 = jnp.float32
    vmem = pl.BlockSpec(memory_space=pltpu.VMEM)
    scratch = (
        [pltpu.VMEM((count * B, B), f32) for count in m_counts]
        + [pltpu.VMEM((rows, B), f32) for _, rows in m_plans]
        + [pltpu.VMEM((count * B, B), f32) for count in m_counts]
        + [pltpu.VMEM((count * B, B), f32) for count in g_counts]
        + [pltpu.VMEM((rows, B), f32) for _, rows in g_plans]
        + [pltpu.VMEM((count * B, B), f32) for count in g_counts]
        + [pltpu.SemaphoreType.DMA((STREAMS, stages))] * 8
    )
    predicted, gram = pl.pallas_call(
        functools.partial(predict_kernel, npw, orders, [p[0] for p in m_plans], [p[0] for p in g_plans]),
        out_shape=(
            jax.ShapeDtypeStruct((norb, width), f32),
            jax.ShapeDtypeStruct((sum(g_counts) * B, B), f32),
        ),
        in_specs=[vmem],
        out_specs=(vmem, vmem),
        scratch_shapes=scratch,
        compiler_params=pltpu.CompilerParams(collective_id=0, has_side_effects=True, vmem_limit_bytes=48 << 20),
    )(history)
    return pl.pallas_call(
        solve_kernel,
        out_shape=jax.ShapeDtypeStruct((norb, width), f32),
        in_specs=[vmem, vmem],
        out_specs=vmem,
        scratch_shapes=[
            pltpu.VMEM((sum(g_counts) * B, B), f32),
            pltpu.VMEM((norb, width), f32),
            pltpu.VMEM((B, 2 * B), f32),
        ],
        compiler_params=pltpu.CompilerParams(vmem_limit_bytes=32 << 20),
    )(predicted, gram)


def solution(mesh):
    return jax.shard_map(
        on_device,
        mesh=mesh,
        in_specs=(P(None, None, ("row", "col")),),
        out_specs=P(None, ("row", "col")),
        check_vma=False,
    )
```

time: 445 us -> 101 us (0.23)
  waiting for transfers between devices: 272 us -> 0 us
  other arithmetic: 121 us -> 0 us
  Pallas kernels: 0 us -> 99.7 us
  matrix products: 19.7 us -> 0 us
  between operations: 16.6 us -> 0.01 us
  local copies, waits for them, and re-layouts: 11.9 us -> 1.13 us
    psum x2 -> x0, waiting for transfers between devices: 272 us -> none  [the longest x1 142 us: on_device(): summed = lax.psum(local_terms, ('row', 'col'))]
    another operation x18 -> x0, other arithmetic: 120 us -> none  [the longest x14 78.9 us: on_device(): factor = jnp.linalg.cholesky(gram / npw_total)]
    pallas_call x0 -> x2, Pallas kernels: none -> 99.7 us  [the longest x1 72.8 us: on_device(): pl.pallas_call(functools.partial(predict_kernel, npw, orders, [p[0] for p...]
    dot_general x7 -> x0, matrix products: 15.9 us -> none  [the longest x3 7.06 us: on_device(): jnp.einsum('ip,jp->ij', newest, history[index], precision=precise)]
    another operation x17 -> x0, local copies, waits for them, and re-layouts: 10.7 us -> none
  transfers between devices with their start and end apart: 2 -> 0, of which waited for: 2 -> 0; matrix products, arithmetic and copies ran while one was open for 0% -> 0% of each run, Pallas kernels for 0% -> 0%
where the time goes in v1:
time: 101 us
  Pallas kernels  99.7 us (99%)
  local copies, waits for them, and re-layouts  1.13 us (1%)
    pallas_call x1, Pallas kernels, on_device(): pl.pallas_call(functools.partial(predict_kernel, npw, orders, [p[0] for p...  72.8 us
    pallas_call x1, Pallas kernels, on_device(): pl.pallas_call(solve_kernel, out_shape=jax.ShapeDtypeStruct((norb, width)...  26.9 us

profile of v1, /device:TPU:0, one launch (start us, length us, event | category | flops | bytes accessed | tf_op | source)
XLA Modules:
  0.0 100.9 jit_solution(6208171283024639211)
XLA Ops:
  0.0 0.0 copy-start
  0.0 1.1 %copy-done = f32[3,512,128]{2,1,0:T(8,128)S(1)} copy-done((f32[3,512,128]{2,1,0:T(8,128)S(1)}, f32[3,512,128]{2,1,0:T(8,128)}, u32[]{:S(2)}) %copy-start) | copy-done | bytes 786456
  1.1 72.8 %shard_map.17 = (f32[512,128]{1,0:T(8,128)S(1)}, f32[1280,128]{1,0:T(8,128)S(1)}) custom-call(f32[3,512,128]{2,1,0:T(8,128)S(1)} %copy-done), custom_call_target="tpu_custom_call" | custom-call | tf_op jit(solution)/shard_map/pallas_call | solution.py:296
  74.0 26.9 %shard_map.18 = f32[512,128]{1,0:T(8,128)} custom-call(f32[512,128]{1,0:T(8,128)S(1)} %get-tuple-element.7.p_ref, f32[1280,128]{1,0:T(8,128)S(1)} %get-tuple-element.8.g_ref), custom_call_target="tpu_custom_call" | custom-call | tf_op jit(solution)/shard_map/pallas_call | solution.py:307
Async XLA Ops:
  0.0 1.1 %copy-start = (f32[3,512,128]{2,1,0:T(8,128)S(1)}, f32[3,512,128]{2,1,0:T(8,128)}, u32[]{:S(2)}) copy-start(f32[3,512,128]{2,1,0:T(8,128)} %h_ref.1) | copy-start | bytes 2359300

commit v2 on v1

--- a/solution.py
+++ b/solution.py
@@ -10,7 +10,8 @@
 
 MESH = pl.DeviceIdType.MESH
 B = 128
-STREAMS = 3
+M_STREAMS, M_HALVINGS = 9, 4
+G_STREAMS, G_HALVINGS = 6, 2
 WEIGHTS = (2.5, -2.0, 0.5)
 NT = (((1,), (1,)), ((), ()))
 NN = (((1,), (0,)), ((), ()))
@@ -26,13 +27,18 @@
     return mul(a[0], b[0]) + (mul(a[0], b[1]) + mul(a[1], b[0]))
 
 
-def exchange_orders(n_row, n_col):
+def exchange_orders(n_row, n_col, streams):
     row = [("row", bit) for bit in range(1, n_row.bit_length() - 1)]
     col = [("col", bit) for bit in range(n_col.bit_length() - 1)]
     half = (len(row) + 1) // 2
-    parts = [row[:half], row[half:], col]
+    inner, outer = row[:half], row[half:]
     first = [("row", 0)]
-    return [first + parts[s] + parts[(s + 1) % 3] + parts[(s + 2) % 3] for s in range(STREAMS)]
+    ways = [
+        inner + outer + col,
+        outer + col[:1] + inner + col[1:],
+        col[:1] + inner + outer + col[1:],
+    ]
+    return [first + ways[s % 3] for s in range(streams)]
 
 
 def plan(rows, stages, halvings):
@@ -46,9 +52,9 @@
     return steps, offset
 
 
-def layout(blocks):
+def layout(blocks, streams):
     place, counts = {}, []
-    for stream, part in enumerate(np.array_split(np.arange(len(blocks)), STREAMS)):
+    for stream, part in enumerate(np.array_split(np.arange(len(blocks)), streams)):
         counts.append(len(part))
         for slot, index in enumerate(part):
             place[blocks[index]] = (stream, slot * B)
@@ -121,6 +127,7 @@
                 halve, rows, _ = self.plans[s][t]
                 if not halve:
                     continue
+                self.gathered(s, t + 1)
                 _, device = self.partner(*self.orders[s][t])
                 here = pl.ds(self.off[s], rows)
                 copy = pltpu.make_async_remote_copy(
@@ -133,29 +140,34 @@
                 )
                 copy.start()
                 self.copies[s] = copy
-            for s in streams:
-                if self.plans[s][t][0]:
-                    self.copies[s].wait()
-                    self.off[s] = self.parent[s][t]
-
-
-def predict_kernel(npw, orders, m_plans, g_plans, h_ref, p_ref, g_ref, *scratch):
-    m_acc, scratch = scratch[:STREAMS], scratch[STREAMS:]
-    m_recv, scratch = scratch[:STREAMS], scratch[STREAMS:]
-    m_sum, scratch = scratch[:STREAMS], scratch[STREAMS:]
-    g_acc, scratch = scratch[:STREAMS], scratch[STREAMS:]
-    g_recv, scratch = scratch[:STREAMS], scratch[STREAMS:]
-    g_sum, sems = scratch[:STREAMS], scratch[STREAMS:]
+        for s in streams:
+            self.gathered(s, 0)
+
+    def gathered(self, s, t):
+        if t < len(self.plans[s]) and self.plans[s][t][0]:
+            self.copies[s].wait()
+            self.off[s] = self.parent[s][t]
+
+
+def predict_kernel(npw, m_orders, g_orders, m_plans, g_plans, h_ref, p_ref, g_ref, *scratch):
+    scratch = list(scratch)
+
+    def take(count):
+        return [scratch.pop(0) for _ in range(count)]
+
+    m_acc, m_recv, m_sum = (take(M_STREAMS) for _ in range(3))
+    g_acc, g_recv, g_sum = (take(G_STREAMS) for _ in range(3))
+    sems = scratch
     nb = h_ref.shape[1] // B
-    m_red = Reducer(m_acc, m_recv, m_sum, *sems[:4], orders, m_plans)
-    g_red = Reducer(g_acc, g_recv, g_sum, *sems[4:], orders, g_plans)
+    m_red = Reducer(m_acc, m_recv, m_sum, *sems[:4], m_orders, m_plans)
+    g_red = Reducer(g_acc, g_recv, g_sum, *sems[4:], g_orders, g_plans)
 
     barrier = pltpu.get_barrier_semaphore()
-    for axis, bit in orders[0]:
+    for axis, bit in m_orders[0]:
         pl.semaphore_signal(barrier, inc=1, device_id=m_red.partner(axis, bit)[1], device_id_type=MESH)
 
     hist = [split(h_ref[j]) for j in range(3)]
-    place, counts = layout(projection_blocks(nb))
+    place, counts = layout(projection_blocks(nb), M_STREAMS)
     left = list(counts)
     waited = False
     for j in range(3):
@@ -170,7 +182,7 @@
                 left[stream] -= 1
                 if left[stream] == 0:
                     if not waited:
-                        pl.semaphore_wait(barrier, len(orders[0]))
+                        pl.semaphore_wait(barrier, len(m_orders[0]))
                         waited = True
                     m_red.start(stream, 0)
     m_red.run()
@@ -182,7 +194,7 @@
         return m_sum[stream][row : row + B, :]
 
     scaled = split(jnp.concatenate([h_ref[j] * (WEIGHTS[j] / npw) for j in range(3)], axis=0))
-    g_place, g_counts = layout(gram_blocks(nb))
+    g_place, g_counts = layout(gram_blocks(nb), G_STREAMS)
     left = list(g_counts)
     highs, lows = [], []
     for i in range(nb):
@@ -202,7 +214,7 @@
                 g_red.start(stream, 0)
     g_red.run()
     row = 0
-    for stream in range(STREAMS):
+    for stream in range(G_STREAMS):
         rows = g_counts[stream] * B
         g_ref[row : row + rows, :] = g_sum[stream][...] * (1.0 / npw)
         row += rows
@@ -215,36 +227,48 @@
     work[:, B:] = jnp.where(rows_of == cols_of, 1.0, 0.0)
     sub = lax.broadcasted_iota(jnp.int32, (8, B), 0)
     inverse = []
-    for k in range(0, B, 8):
-        left, right = work[k : k + 8, :B], work[k : k + 8, B:]
-        cols = [jnp.broadcast_to(left[:, k + r : k + r + 1], (8, B)) for r in range(8)]
-        pivots = None
-        for r in range(8):
-            def line(x):
-                return jnp.broadcast_to(x[r : r + 1, :], (8, B))
-
-            pivot = line(cols[r])
-            pivots = pivot if r == 0 else jnp.where(sub == r, pivot, pivots)
-            if r < 7:
-                scale = jnp.where(sub > r, cols[r] / pivot, 0.0)
-                for s in range(r + 1, 8):
-                    cols[s] = cols[s] - scale * line(cols[s])
-                left = left - scale * line(left)
-                right = right - scale * line(right)
-        root = 1.0 / jnp.sqrt(pivots)
-        left, right = left * root, right * root
+
+    def line(x, r):
+        return jnp.broadcast_to(x[r : r + 1, :], (8, B))
+
+    for k in range(0, B, 16):
+        top = [jnp.broadcast_to(work[k : k + 8, k + r : k + r + 1], (8, B)) for r in range(16)]
+        low = [jnp.broadcast_to(work[k + 8 : k + 16, k + r : k + r + 1], (8, B)) for r in range(16)]
+        top += [work[k : k + 8, :B], work[k : k + 8, B:]]
+        low += [work[k + 8 : k + 16, :B], work[k + 8 : k + 16, B:]]
+        pivots = [None, None]
+        for r in range(16):
+            upper, q = r < 8, r % 8
+            pivot = line((top if upper else low)[r], q)
+            pivots[r // 8] = pivot if q == 0 else jnp.where(sub == q, pivot, pivots[r // 8])
+            if r == 15:
+                break
+            inv = 1.0 / pivot
+            if upper:
+                top_scale = jnp.where(sub > q, top[r] * inv, 0.0)
+                low_scale = low[r] * inv
+                for s in range(r + 1, 18):
+                    row = line(top[s], q)
+                    top[s] = top[s] - top_scale * row
+                    low[s] = low[s] - low_scale * row
+            else:
+                low_scale = jnp.where(sub > q, low[r] * inv, 0.0)
+                for s in range(r + 1, 18):
+                    low[s] = low[s] - low_scale * line(low[s], q)
+        root = [1.0 / jnp.sqrt(p) for p in pivots]
+        left = jnp.concatenate([top[16] * root[0], low[16] * root[1]], axis=0)
+        right = jnp.concatenate([top[17] * root[0], low[17] * root[1]], axis=0)
         inverse.append(right)
-        if k + 8 < B:
+        if k + 16 < B:
             lh = left.astype(jnp.bfloat16).astype(jnp.float32)
             rh = right.astype(jnp.bfloat16).astype(jnp.float32)
             ll, rl = left - lh, right - rh
-            zero = jnp.zeros_like(lh)
-            tall = jnp.transpose(jnp.concatenate([lh, ll, lh, zero], axis=0)).astype(jnp.bfloat16)
+            tall = jnp.transpose(jnp.concatenate([lh, ll, lh], axis=0)).astype(jnp.bfloat16)
             wide = jnp.concatenate(
-                [jnp.concatenate([lh, lh, ll, zero], axis=0), jnp.concatenate([rh, rh, rl, zero], axis=0)], axis=1
+                [jnp.concatenate([lh, lh, ll], axis=0), jnp.concatenate([rh, rh, rl], axis=0)], axis=1
             ).astype(jnp.bfloat16)
             update = lax.dot_general(tall, wide, NN, preferred_element_type=jnp.float32)
-            work[k + 8 :, :] = work[k + 8 :, :] - update[k + 8 :, :]
+            work[k + 16 :, :] = work[k + 16 :, :] - update[k + 16 :, :]
     return jnp.concatenate(inverse, axis=0)
 
 
@@ -276,12 +300,13 @@
     norb, width = history.shape[1:]
     npw = width * n_row * n_col
     nb = norb // B
-    orders = exchange_orders(n_row, n_col)
-    stages = len(orders[0])
-    m_counts = layout(projection_blocks(nb))[1]
-    g_counts = layout(gram_blocks(nb))[1]
-    m_plans = [plan(count * B, stages, 4) for count in m_counts]
-    g_plans = [plan(count * B, stages, 2) for count in g_counts]
+    m_orders = exchange_orders(n_row, n_col, M_STREAMS)
+    g_orders = exchange_orders(n_row, n_col, G_STREAMS)
+    stages = len(m_orders[0])
+    m_counts = layout(projection_blocks(nb), M_STREAMS)[1]
+    g_counts = layout(gram_blocks(nb), G_STREAMS)[1]
+    m_plans = [plan(count * B, stages, M_HALVINGS) for count in m_counts]
+    g_plans = [plan(count * B, stages, G_HALVINGS) for count in g_counts]
     f32 = jnp.float32
     vmem = pl.BlockSpec(memory_space=pltpu.VMEM)
     scratch = (
@@ -291,10 +316,11 @@
         + [pltpu.VMEM((count * B, B), f32) for count in g_counts]
         + [pltpu.VMEM((rows, B), f32) for _, rows in g_plans]
         + [pltpu.VMEM((count * B, B), f32) for count in g_counts]
-        + [pltpu.SemaphoreType.DMA((STREAMS, stages))] * 8
+        + [pltpu.SemaphoreType.DMA((M_STREAMS, stages))] * 4
+        + [pltpu.SemaphoreType.DMA((G_STREAMS, stages))] * 4
     )
     predicted, gram = pl.pallas_call(
-        functools.partial(predict_kernel, npw, orders, [p[0] for p in m_plans], [p[0] for p in g_plans]),
+        functools.partial(predict_kernel, npw, m_orders, g_orders, [p[0] for p in m_plans], [p[0] for p in g_plans]),
         out_shape=(
             jax.ShapeDtypeStruct((norb, width), f32),
             jax.ShapeDtypeStruct((sum(g_counts) * B, B), f32),

time: 101 us -> 84.2 us (0.83)
  Pallas kernels: 99.7 us -> 82.9 us
    pallas_call x1, Pallas kernels: 26.9 us -> 17.5 us  [on_device(): pl.pallas_call(solve_kernel, out_shape=jax.ShapeDtypeStruct((norb, width)...]
    pallas_call x1, Pallas kernels: 72.8 us -> 65.4 us  [on_device(): pl.pallas_call(functools.partial(predict_kernel, npw, m_orders, g_orders,...]
where the time goes in v2:
time: 84.2 us; the launch traced here: 84 us
  Pallas kernels  82.9 us (98%)
  local copies, waits for them, and re-layouts  1.13 us (1%)
    pallas_call x1, Pallas kernels, on_device(): pl.pallas_call(functools.partial(predict_kernel, npw, m_orders, g_orders,...  65.4 us
    pallas_call x1, Pallas kernels, on_device(): pl.pallas_call(solve_kernel, out_shape=jax.ShapeDtypeStruct((norb, width)...  17.5 us

profile of v2, /device:TPU:0, one launch (start us, length us, event | category | flops | bytes accessed | tf_op | source)
XLA Modules:
  0.0 84.0 jit_solution(15818134025821051601)
XLA Ops:
  0.0 0.0 copy-start
  0.0 1.1 %copy-done = f32[3,512,128]{2,1,0:T(8,128)S(1)} copy-done((f32[3,512,128]{2,1,0:T(8,128)S(1)}, f32[3,512,128]{2,1,0:T(8,128)}, u32[]{:S(2)}) %copy-start) | copy-done | bytes 786456
  1.1 65.4 %shard_map.17 = (f32[512,128]{1,0:T(8,128)S(1)}, f32[1280,128]{1,0:T(8,128)S(1)}) custom-call(f32[3,512,128]{2,1,0:T(8,128)S(1)} %copy-done), custom_call_target="tpu_custom_call" | custom-call | tf_op jit(solution)/shard_map/pallas_call | solution.py:322
  66.5 17.5 %shard_map.18 = f32[512,128]{1,0:T(8,128)} custom-call(f32[512,128]{1,0:T(8,128)S(1)} %get-tuple-element.7.p_ref, f32[1280,128]{1,0:T(8,128)S(1)} %get-tuple-element.8.g_ref), custom_call_target="tpu_custom_call" | custom-call | tf_op jit(solution)/shard_map/pallas_call | solution.py:333
Async XLA Ops:
  0.0 1.1 %copy-start = (f32[3,512,128]{2,1,0:T(8,128)S(1)}, f32[3,512,128]{2,1,0:T(8,128)}, u32[]{:S(2)}) copy-start(f32[3,512,128]{2,1,0:T(8,128)} %h_ref.1) | copy-start | bytes 2359300
